TPU v7x, 32 devices: a whole 2x2x4 slice. The times are simulated.
32 devices in a mesh: island: 16 (over z, y, x), tensor: 2 (over core).
Axes of the slice: x: 2, y: 2, z: 4, core: 2. Of those that a mesh axis runs over, the one named last changes fastest.
Arguments:
- pseudo_grad: float32 [16, 32, 53248], P('island', None, 'tensor'), may hold values from -8000 to 8000
- outer_params: float32 [32, 53248], P('island', 'tensor'), may hold values from -4 to 4
- momentum: float32 [32, 53248], P('island', 'tensor'), may hold values from -6 to 6
- save_pages: int32 [16], replicated, may hold values from 1 to 832, 6656 in all
- writer: int32 [16], replicated, may hold values from 0 to 15, each once
Outputs:
- new_master: float32 [32, 53248], P('island', 'tensor')
- new_momentum: float32 [32, 53248], P('island', 'tensor')
- checkpoint: bfloat16 [16, 832, 256], P('island', None, 'tensor')
Inputs may be any that keep to these rules, and one draw needn't show every extreme that they name: save_pages sums to 6656; the longest range has exactly 832 pages. writer names every island once.
All inputs are finite; a program needn't handle non-finite values.
Results may differ from a plain program's by a relative error of at most 0.0007.
Values may be sent and summed in bfloat16 or wider, within the bound.
A program may use at most 64 MiB of HBM per device.

v0:
```python
import jax
import jax.numpy as jnp
from jax import lax
from jax.sharding import PartitionSpec as P

epsilon = 1e-06
decay_rate = 0.9
outer_rate = 0.7


def body(pseudo_grad, outer_params, momentum, save_pages, writer):
    own_rows = outer_params.shape[0]
    col_width = outer_params.shape[1]
    islands = lax.axis_size("island")
    my_index = lax.axis_index("island")
    own_grad = pseudo_grad[0]
    entries = own_grad.shape[0] * col_width * lax.axis_size("tensor")
    summed = lax.psum(own_grad, "island")
    full_grad = summed / islands
    square_sum = lax.psum(jnp.sum(full_grad * full_grad), "tensor")
    outer_grad = lax.dynamic_slice_in_dim(full_grad, my_index * own_rows, own_rows, 0)
    normed = outer_grad / jnp.sqrt(square_sum / entries + epsilon)
    new_momentum = decay_rate * momentum + normed
    new_master = outer_params - outer_rate * (normed + decay_rate * new_momentum)
    cast_rows = new_master.astype(jnp.bfloat16)
    pages_own = own_rows * col_width // 128
    capacity = 2 * pages_own
    starts = jnp.cumsum(save_pages) - save_pages
    targets = jnp.arange(islands, dtype=jnp.int32)
    owner_table = writer[None, :] == targets[:, None]
    range_start = jnp.sum(jnp.where(owner_table, starts[None, :], 0), axis=1)
    range_length = jnp.sum(jnp.where(owner_table, save_pages[None, :], 0), axis=1)
    is_mine = targets == my_index
    own_start = jnp.sum(jnp.where(is_mine, range_start, 0))
    own_length = jnp.sum(jnp.where(is_mine, range_length, 0))
    slot_ids = jnp.arange(capacity, dtype=jnp.int32)
    own_pages = cast_rows.reshape(pages_own, 128)
    spread_slots = -(-pages_own // islands)
    deliver_slots = -(-capacity // islands)
    spread_ids = jnp.arange(spread_slots, dtype=jnp.int32)
    offset = jnp.mod(targets - my_index * pages_own, islands)
    local_index = offset[:, None] + islands * spread_ids[None, :]
    live_slot = (local_index < pages_own).reshape(-1, 1)
    outgoing = jnp.take(own_pages, jnp.clip(local_index, 0, pages_own - 1).reshape(-1), axis=0)
    outgoing = jnp.where(live_slot, outgoing, jnp.zeros_like(outgoing))
    spread = lax.all_to_all(outgoing, "island", split_axis=0, concat_axis=0, tiled=True)
    deliver_ids = jnp.arange(deliver_slots, dtype=jnp.int32)
    first_page = range_start + jnp.mod(my_index - range_start, islands)
    global_page = first_page[:, None] + islands * deliver_ids[None, :]
    live_out = (global_page < (range_start + range_length)[:, None]).reshape(-1, 1)
    held_index = (
        global_page // pages_own * spread_slots + jnp.mod(global_page, pages_own) // islands
    )
    held_index = jnp.clip(held_index, 0, islands * spread_slots - 1).reshape(-1)
    forward = jnp.take(spread, held_index, axis=0)
    forward = jnp.where(live_out, forward, jnp.zeros_like(forward))
    delivered = lax.all_to_all(forward, "island", split_axis=0, concat_axis=0, tiled=True)
    source = jnp.mod(own_start + slot_ids, islands) * deliver_slots + slot_ids // islands
    source = jnp.clip(source, 0, islands * deliver_slots - 1)
    packed = jnp.take(delivered, source, axis=0)
    packed = jnp.where((slot_ids < own_length)[:, None], packed, jnp.zeros_like(packed))
    return (new_master, new_momentum, packed[None])


def solution(mesh):
    in_specs = (P("island", None, "tensor"), P("island", "tensor"), P("island", "tensor"), P(), P())
    out_specs = (P("island", "tensor"), P("island", "tensor"), P("island", None, "tensor"))
    return jax.shard_map(body, mesh=mesh, in_specs=in_specs, out_specs=out_specs, check_vma=False)
```

profile of v0, /device:TPU:0, one launch (start us, length us, event | category | flops | bytes accessed | tf_op | source)
XLA Modules:
  0.0 218.6 jit_solution(9376555139836277744)
XLA Ops:
  7.2 0.0 copy-start
  7.2 0.0 copy-start.1
  7.2 0.0 all-reduce.2.cloned.1.call-start
  7.2 0.7 all-reduce.2.cloned.1.call-update
  8.0 0.1 add_clamp_fusion
  8.0 0.1 min.40
  8.1 0.0 copy-done
  8.1 0.1 copy.10
  8.3 0.1 reduce
  8.4 0.0 copy-done.1
  8.4 0.1 select_reduce_fusion.1
  8.5 0.7 fusion.32
  9.2 0.1 add_divide_fusion
  9.3 0.1 rem.175
  9.4 0.1 div.75
  9.5 0.1 add_compare_fusion
  9.6 0.1 ne.202
  9.7 0.1 add_compare_fusion.1
  9.8 159.0 %all-reduce.2.cloned.1.call-done = f32[32,26624]{1,0:T(8,128)} async-done(((f32[32,26624]{1,0:T(8,128)}), f32[32,26624]{1,0:T(8,128)}) %all-reduce.2.cloned.1.call-update) | async-done | bytes 3407888 | tf_op jit(solution)/shard_map/psum | solution.py:18
  168.8 3.5 %broadcast_multiply_fusion = (f32[32,26624]{1,0:T(8,128)S(1)}, f32[]{:T(128)}) fusion(f32[32,26624]{1,0:T(8,128)} %all-reduce.2.cloned.1.call-done), kind=kLoop, calls=%fused_computation.4 | loop fusion | flops 2555903 | bytes 6815748 | tf_op jit(solution)/shard_map/div | solution.py:19
  172.2 3.1 %psum.15 = f32[]{:T(128)} all-reduce(f32[]{:T(128)} %get-tuple-element.9), channel_id=1, replica_groups=mesh['island'=16,'tensor'=2] {'tensor'}, use_global_device_ids=true, to_apply=%region_2.0 | all-reduce | flops 1 | bytes 8 | tf_op jit(solution)/shard_map/psum | solution.py:20
  176.0 2.1 fusion.36
  178.1 0.1 reshape.458
  178.2 1.5 gather_fusion
  179.7 0.9 select_select_fusion.1
  180.6 4.7 %all-to-all-start = ((bf16[16,26,128]{2,1,0:T(8,128)(2,1)}), bf16[16,26,128]{2,1,0:T(8,128)(2,1)S(1)}, u32[]{:S(2)}, u32[]{:S(2)}) async-start(bf16[16,26,128]{2,1,0:T(8,128)(2,1)} %select_select_fusion.1), calls=%async_computation | async-start | bytes 262144 | tf_op jit(solution)/shard_map/all_to_all | solution.py:46
  185.3 0.1 fusion.25
  185.4 7.7 %all-to-all-done = bf16[16,26,128]{2,1,0:T(8,128)(2,1)S(1)} async-done(((bf16[16,26,128]{2,1,0:T(8,128)(2,1)}), bf16[16,26,128]{2,1,0:T(8,128)(2,1)S(1)}, u32[]{:S(2)}, u32[]{:S(2)}) %all-to-all-start) | async-done | bytes 106528 | tf_op jit(solution)/shard_map/all_to_all | solution.py:46
  193.1 2.4 %gather_fusion.1 = bf16[832,128]{1,0:T(8,128)(2,1)S(1)} fusion(bf16[416,128]{1,0:T(8,128)(2,1)S(1)} %all_to_all.13, s32[1024]{0:T(1024)S(1)} %pad_clamp_fusion.1), kind=kCustom, calls=%fused_computation.1 | custom fusion | bytes 429312 | tf_op jit(solution)/shard_map/jit(_take)/gather | solution.py:55
  195.5 1.0 select_select_fusion
  196.5 3.5 %all-to-all-start.1 = ((bf16[16,52,128]{2,1,0:T(8,128)(2,1)}), bf16[16,52,128]{2,1,0:T(8,128)(2,1)S(1)}, u32[]{:S(2)}, u32[]{:S(2)}) async-start(bf16[16,52,128]{2,1,0:T(8,128)(2,1)} %select_select_fusion), calls=%async_computation.1 | async-start | bytes 458752 | tf_op jit(solution)/shard_map/all_to_all | solution.py:57
  200.1 0.7 fusion.26
  200.8 1.3 iota_compare_fusion.1
  202.1 6.3 %all-to-all-done.1 = bf16[16,52,128]{2,1,0:T(8,128)(2,1)S(1)} async-done(((bf16[16,52,128]{2,1,0:T(8,128)(2,1)}), bf16[16,52,128]{2,1,0:T(8,128)(2,1)S(1)}, u32[]{:S(2)}, u32[]{:S(2)}) %all-to-all-start.1) | async-done | bytes 213024 | tf_op jit(solution)/shard_map/all_to_all | solution.py:57
  208.4 2.4 %gather_fusion.2 = bf16[832,128]{1,0:T(8,128)(2,1)S(1)} fusion(bf16[832,128]{1,0:T(8,128)(2,1)S(1)} %all_to_all.15, s32[1024]{0:T(1024)S(1)} %pad_clamp_fusion), kind=kCustom, calls=%fused_computation.2 | custom fusion | bytes 429312 | tf_op jit(solution)/shard_map/jit(_take)/gather | solution.py:60
  210.8 1.0 fusion
  (13 shorter events, 0.2 us)
Async XLA Ops:
  7.2 1.0 copy-start
  7.2 1.2 copy-start.1
  7.2 161.6 %all-reduce.2.cloned.1.call-start = ((), (), s32[]{:S(2)}) async-start(), calls=%async_computation.2 | async-start | bytes 6815744 | tf_op jit(solution)/shard_map/psum | solution.py:18
  180.6 12.5 %all-to-all-start = ((bf16[16,26,128]{2,1,0:T(8,128)(2,1)}), bf16[16,26,128]{2,1,0:T(8,128)(2,1)S(1)}, u32[]{:S(2)}, u32[]{:S(2)}) async-start(bf16[16,26,128]{2,1,0:T(8,128)(2,1)} %select_select_fusion.1), calls=%async_computation | async-start | bytes 262144 | tf_op jit(solution)/shard_map/all_to_all | solution.py:46
  196.5 11.8 %all-to-all-start.1 = ((bf16[16,52,128]{2,1,0:T(8,128)(2,1)}), bf16[16,52,128]{2,1,0:T(8,128)(2,1)S(1)}, u32[]{:S(2)}, u32[]{:S(2)}) async-start(bf16[16,52,128]{2,1,0:T(8,128)(2,1)} %select_select_fusion), calls=%async_computation.1 | async-start | bytes 458752 | tf_op jit(solution)/shard_map/all_to_all | solution.py:57
Sparse Core Ops, SparseCore 0:
  13.7 155.0 all-reduce.1
where the time goes:
time: 219 us
  waiting for transfers between devices  174 us (79%)
  between operations  14.9 us (7%)
  other arithmetic  11.8 us (5%)
  starting transfers between devices  8.25 us (4%)
  local copies, waits for them, and re-layouts  6.87 us (3%)
  blocking collectives  3.08 us (1%)
    psum x1, waiting for transfers between devices, body(): summed = lax.psum(own_grad, 'island')  159 us
    all_to_all x1, waiting for transfers between devices, body(): lax.all_to_all(outgoing, 'island', split_axis=0, concat_axis=0, tiled=True)  7.72 us
    all_to_all x1, waiting for transfers between devices, body(): lax.all_to_all(forward, 'island', split_axis=0, concat_axis=0, tiled=True)  6.3 us
    all_to_all x1, starting transfers between devices, body(): lax.all_to_all(outgoing, 'island', split_axis=0, concat_axis=0, tiled=True)  4.69 us
  transfers between devices with their start and end apart: 3, of which 3 were waited for; matrix products, arithmetic and copies ran while one was open for 2% of the time, Pallas kernels for 0%

commit v1 on v0

--- a/solution.py
+++ b/solution.py
@@ -15,7 +15,7 @@
     my_index = lax.axis_index("island")
     own_grad = pseudo_grad[0]
     entries = own_grad.shape[0] * col_width * lax.axis_size("tensor")
-    summed = lax.psum(own_grad, "island")
+    summed = jnp.sum(lax.all_gather(own_grad, "island"), axis=0)
     full_grad = summed / islands
     square_sum = lax.psum(jnp.sum(full_grad * full_grad), "tensor")
     outer_grad = lax.dynamic_slice_in_dim(full_grad, my_index * own_rows, own_rows, 0)

time: 219 us -> 628 us (2.87)
  waiting for transfers between devices: 174 us -> 567 us
  other arithmetic: 11.8 us -> 28.8 us
    all_gather x0 -> x1, waiting for transfers between devices: none -> 552 us  [body(): summed = jnp.sum(lax.all_gather(own_grad, 'island'), axis=0)]
    psum x1 -> x0, waiting for transfers between devices: 159 us -> none  [body(): summed = lax.psum(own_grad, 'island')]
    reduce_sum x0 -> x1, other arithmetic: none -> 17.3 us  [body(): summed = jnp.sum(lax.all_gather(own_grad, 'island'), axis=0)]
  transfers between devices with their start and end apart: 3 -> 3, of which waited for: 3 -> 3; matrix products, arithmetic and copies ran while one was open for 2% -> 1% of each run, Pallas kernels for 0% -> 0%
where the time goes in v1:
time: 628 us
  waiting for transfers between devices  567 us (90%)
  other arithmetic  28.8 us (5%)
  between operations  14.9 us (2%)
  starting transfers between devices  7.37 us (1%)
  local copies, waits for them, and re-layouts  6.87 us (1%)
    all_gather x1, waiting for transfers between devices, body(): summed = jnp.sum(lax.all_gather(own_grad, 'island'), axis=0)  552 us
    reduce_sum x1, other arithmetic, body(): summed = jnp.sum(lax.all_gather(own_grad, 'island'), axis=0)  17.3 us
  transfers between devices with their start and end apart: 3, of which 3 were waited for; matrix products, arithmetic and copies ran while one was open for 1% of the time, Pallas kernels for 0%

profile of v1, /device:TPU:0, one launch (start us, length us, event | category | flops | bytes accessed | tf_op | source)
XLA Modules:
  0.0 627.9 jit_solution(5933027979545774331)
XLA Ops:
  7.2 0.0 copy-start
  7.2 0.0 copy-start.1
  7.2 0.0 all-gather.2.cloned.1.call-start
  7.2 0.7 all-gather.2.cloned.1.call-update
  8.0 0.1 add_clamp_fusion
  8.0 0.1 min.40
  8.1 0.0 copy-done
  8.1 0.1 copy.11
  8.3 0.1 reduce
  8.4 0.0 copy-done.1
  8.4 0.1 select_reduce_fusion.1
  8.5 0.7 fusion.32
  9.2 0.1 add_divide_fusion
  9.2 0.1 rem.175
  9.3 0.1 div.75
  9.4 0.1 add_compare_fusion
  9.5 0.1 ne.202
  9.7 0.1 add_compare_fusion.1
  9.7 552.0 %all-gather.2.cloned.1.call-done = f32[16,32,26624]{2,1,0:T(8,128)} async-done(((f32[1,32,26624]{2,1,0:T(8,128)}), f32[16,32,26624]{2,1,0:T(8,128)}) %all-gather.2.cloned.1.call-update) | async-done | bytes 54525968 | tf_op jit(solution)/shard_map/all_gather | solution.py:18
  561.8 17.3 %reduce_sum.54 = f32[32,26624]{1,0:T(8,128)S(1)} reduce(f32[16,32,26624]{2,1,0:T(8,128)} %all-gather.2.cloned.1.call-done, f32[]{:T(128)} %constant.127.clone.1), dimensions={0}, to_apply=%region_0.0 | reduce | flops 12779520 | bytes 57933828 | tf_op jit(solution)/shard_map/reduce_sum | solution.py:18
  579.0 3.1 broadcast_multiply_fusion
  582.2 3.1 psum.7
  586.0 2.3 fusion.36
  588.3 0.1 reshape.458
  588.4 1.5 gather_fusion
  589.9 0.9 select_select_fusion.1
  590.8 3.8 all-to-all-start
  594.6 0.1 fusion.25
  594.6 7.7 %all-to-all-done = bf16[16,26,128]{2,1,0:T(8,128)(2,1)S(1)} async-done(((bf16[16,26,128]{2,1,0:T(8,128)(2,1)}), bf16[16,26,128]{2,1,0:T(8,128)(2,1)S(1)}, u32[]{:S(2)}, u32[]{:S(2)}) %all-to-all-start) | async-done | bytes 106528 | tf_op jit(solution)/shard_map/all_to_all | solution.py:46
  602.4 2.4 gather_fusion.1
  604.8 1.0 select_select_fusion
  605.8 3.5 all-to-all-start.1
  609.3 0.7 fusion.26
  610.0 1.2 iota_compare_fusion.1
  611.2 6.4 %all-to-all-done.1 = bf16[16,52,128]{2,1,0:T(8,128)(2,1)S(1)} async-done(((bf16[16,52,128]{2,1,0:T(8,128)(2,1)}), bf16[16,52,128]{2,1,0:T(8,128)(2,1)S(1)}, u32[]{:S(2)}, u32[]{:S(2)}) %all-to-all-start.1) | async-done | bytes 213024 | tf_op jit(solution)/shard_map/all_to_all | solution.py:57
  617.7 2.4 gather_fusion.2
  620.1 1.0 fusion
  (13 shorter events, 0.2 us)
Async XLA Ops:
  7.2 1.0 copy-start
  7.2 1.2 copy-start.1
  7.2 554.6 %all-gather.2.cloned.1.call-start = ((), (), s32[]{:S(2)}) async-start(), calls=%async_computation.2 | async-start | bytes 57933824 | tf_op jit(solution)/shard_map/all_gather | solution.py:18
  590.8 11.6 %all-to-all-start = ((bf16[16,26,128]{2,1,0:T(8,128)(2,1)}), bf16[16,26,128]{2,1,0:T(8,128)(2,1)S(1)}, u32[]{:S(2)}, u32[]{:S(2)}) async-start(bf16[16,26,128]{2,1,0:T(8,128)(2,1)} %select_select_fusion.1), calls=%async_computation | async-start | bytes 262144 | tf_op jit(solution)/shard_map/all_to_all | solution.py:46
  605.8 11.8 %all-to-all-start.1 = ((bf16[16,52,128]{2,1,0:T(8,128)(2,1)}), bf16[16,52,128]{2,1,0:T(8,128)(2,1)S(1)}, u32[]{:S(2)}, u32[]{:S(2)}) async-start(bf16[16,52,128]{2,1,0:T(8,128)(2,1)} %select_select_fusion), calls=%async_computation.1 | async-start | bytes 458752 | tf_op jit(solution)/shard_map/all_to_all | solution.py:57
Sparse Core Ops, SparseCore 0:
  10.7 551.0 all-gather.1
